TPU v7x, 512 devices: a whole 4x8x8 slice. The times are simulated.
512 devices in a mesh: group: 2 (over core), dp: 64 (over y, x, z_hi), mp: 4 (over z_lo).
Axes of the slice: x: 4, y: 8, z: 8 (z_hi: 2, z_lo: 4; z = z_hi * 4 + z_lo), core: 2. Of those that a mesh axis runs over, the one named last changes fastest.
Arguments:
- x_arrive: bfloat16 [256, 256, 1152], P(('group', 'dp')), may hold values from -6 to 6
- cond_first: int32 [128], P(('group', 'dp')), may hold values 0 or 1
- labels: int32 [128], P(('group', 'dp')), may hold values from 0 to 999
- step_ids: int32 [128], P(('group', 'dp')), may hold values from 0 to 999
- guidance: float32 [1], replicated, may hold values from 2 to 6
- time_table: bfloat16 [1000, 1152], P(None, 'mp'), may hold values from -6 to 6
- class_table: bfloat16 [1001, 1152], P(None, 'mp'), may hold values from -6 to 6
- ada_weight: bfloat16 [1152, 6912], P('mp', 'dp'), may hold values from -0.1875 to 0.1875
- final_ada: bfloat16 [1152, 2304], P('mp'), may hold values from -0.1875 to 0.1875
- qkv_weight: bfloat16 [3, 1152, 1152], P(None, 'dp', 'mp'), may hold values from -2 to 2
- proj_weight: bfloat16 [1152, 1152], P('mp', 'dp'), may hold values from -0.1875 to 0.1875
- fc1_weight: bfloat16 [1152, 4608], P('dp', 'mp'), may hold values from -0.1875 to 0.1875
- fc2_weight: bfloat16 [4608, 1152], P('mp', 'dp'), may hold values from -0.09375 to 0.09375
- out_weight: bfloat16 [1152, 16], replicated, may hold values from -0.1875 to 0.1875
Outputs:
- guided: float32 [128, 4096], P(('group', 'dp'), 'mp')
All inputs are finite; a program needn't handle non-finite values. No bound on the sum of `cond_first` on one device may be relied on, other than what follows from the above.
Results may differ from a plain program's by a relative error of at most 0.025.
Values may be sent and summed in bfloat16 or wider, within the bound.
No kernel may reach another device: no remote copies, remote signals or barrier semaphores. Data moves between devices by JAX's collectives and lax.ppermute only.
A program may use at most 64 MiB of HBM per device.

v0:
```python
import jax
import jax.numpy as jnp
from jax import lax
from jax.sharding import Mesh
from jax.sharding import PartitionSpec as P

HEADS = 16
CLASSES = 1000
DP = ("dp_0", "dp_1", "dp_2")
GROUP_DP = ("group", "dp_0", "dp_1", "dp_2")


def from_everyone(x, axis):
    size = lax.axis_size(axis)
    return lax.all_to_all(jnp.broadcast_to(x[None], (size, *x.shape)), axis, 0, 0, tiled=True)


def laid_out(pieces, dim):
    pieces = jnp.moveaxis(pieces, 0, dim)
    shape = pieces.shape
    return pieces.reshape(*shape[:dim], shape[dim] * shape[dim + 1], *shape[dim + 2 :])


def collect(x, axis, dim):
    pieces = from_everyone(x, axis)
    return laid_out(pieces, dim)


def of_everyone(x, axis):
    everything = from_everyone(x, axis)
    return jnp.sum(everything.astype(jnp.float32), axis=0)


def gathered_by_axis(x, axes, dim):
    for axis in reversed(axes):
        x = lax.all_gather(x, axis, axis=dim, tiled=True)
    return x


def cut_along(x, dim, size):
    shape = x.shape
    pieces = x.reshape(*shape[:dim], size, shape[dim] // size, *shape[dim + 1 :])
    return jnp.moveaxis(pieces, dim, 0)


def sum_at_owner(x, axis, dim):
    size = lax.axis_size(axis)
    pieces = lax.all_to_all(cut_along(x, dim, size), axis, 0, 0, tiled=True)
    return jnp.sum(pieces.astype(jnp.float32), axis=0)


def layer_norm(values):
    mean = jnp.mean(values, axis=-1, keepdims=True)
    centred = values - mean
    spread = jnp.mean(centred * centred, axis=-1, keepdims=True)
    return centred * lax.rsqrt(spread + 1e-06)


def on_device(
    x_arrive,
    cond_first,
    labels,
    step_ids,
    guidance,
    time_table,
    class_table,
    ada_weight,
    final_ada,
    qkv_weight,
    proj_weight,
    fc1_weight,
    fc2_weight,
    out_weight,
):
    pair_count = labels.shape[0]
    tokens = x_arrive.shape[1]
    width = x_arrive.shape[2]
    image_count = 2 * pair_count
    row_count = image_count * tokens
    split_rows = x_arrive.reshape(pair_count, 2, tokens, width)
    first = (cond_first == 1)[:, None, None]
    cond_rows = jnp.where(first, split_rows[:, 0], split_rows[:, 1])
    uncond_rows = jnp.where(first, split_rows[:, 1], split_rows[:, 0])
    x_sides = jnp.stack([cond_rows, uncond_rows])
    time_part = jnp.take(time_table, step_ids, axis=0).astype(jnp.float32)
    class_part = jnp.take(class_table, labels, axis=0).astype(jnp.float32)
    null_part = class_table[CLASSES].astype(jnp.float32)[None, :]
    emb_sides = time_part[None] + jnp.stack([class_part, null_part])
    act_sides = jax.nn.silu(emb_sides).astype(jnp.bfloat16)
    images, acts = (x_sides, act_sides)
    images = images.reshape(image_count, tokens, width)
    acts = acts.reshape(image_count, act_sides.shape[2])
    partial_final = jnp.dot(acts, final_ada, preferred_element_type=jnp.float32)
    every_act = collect(acts, DP, 0)
    column_part = jnp.dot(every_act, ada_weight, preferred_element_type=jnp.float32)
    summed, fmods = (
        of_everyone(column_part.astype(jnp.bfloat16), "mp").astype(jnp.float32),
        of_everyone(partial_final.astype(jnp.bfloat16), "mp").astype(jnp.float32),
    )
    mods = lax.all_to_all(
        summed.astype(jnp.bfloat16), DP, split_axis=0, concat_axis=1, tiled=True
    ).astype(summed.dtype)
    shift_a, scale_a, gate_a, shift_m, scale_m, gate_m = jnp.split(mods, 6, axis=1)
    shift_f, scale_f = jnp.split(fmods, 2, axis=1)
    images_f = images.astype(jnp.float32)
    hidden = (layer_norm(images_f) * (1.0 + scale_a[:, None]) + shift_a[:, None]).astype(
        jnp.bfloat16
    )
    hidden = hidden.reshape(row_count, width)
    quarter = qkv_weight.shape[2]
    head_dim = width // HEADS
    local_heads = quarter // head_dim
    columns = hidden
    qkv = jnp.einsum(
        "rd,kdc->krc",
        columns,
        lax.all_gather(qkv_weight, DP, axis=1, tiled=True),
        preferred_element_type=jnp.float32,
    ).astype(jnp.bfloat16)
    query = qkv[0].reshape(image_count, tokens, local_heads, head_dim)
    keys = qkv[1].reshape(image_count, tokens, local_heads, head_dim)
    values = qkv[2].reshape(image_count, tokens, local_heads, head_dim)
    scores = jnp.einsum(
        "bqhe,bkhe->bhqk", query, keys, preferred_element_type=jnp.float32
    ) * head_dim ** (-0.5)
    probs = jax.nn.softmax(scores, axis=-1).astype(jnp.bfloat16)
    mixed = jnp.einsum("bhqk,bkhe->bqhe", probs, values, preferred_element_type=jnp.float32).astype(
        jnp.bfloat16
    )
    mixed = mixed.reshape(row_count, quarter)
    attn_part = jnp.dot(mixed, collect(proj_weight, DP, 1), preferred_element_type=jnp.float32)
    attn = (
        lax.psum(attn_part.astype(jnp.bfloat16), "mp")
        .astype(jnp.float32)
        .reshape(image_count, tokens, width)
    )
    first_sum = images_f + gate_a[:, None] * attn
    hidden_two = (layer_norm(first_sum) * (1.0 + scale_m[:, None]) + shift_m[:, None]).astype(
        jnp.bfloat16
    )
    hidden_two = hidden_two.reshape(row_count, width)
    ff_quarter = fc1_weight.shape[1]
    columns = hidden_two
    up = jnp.dot(columns, gathered_by_axis(fc1_weight, DP, 0), preferred_element_type=jnp.float32)
    gelu_h = (
        jax.nn.gelu(up, approximate=True)
        .astype(jnp.bfloat16)
        .reshape(image_count, tokens, ff_quarter)
    )
    down_full = gathered_by_axis(fc2_weight, DP, 1)
    token_share = tokens // lax.axis_size("mp")
    mlp = sum_at_owner(
        jnp.einsum("btf,fd->tbd", gelu_h, down_full, preferred_element_type=jnp.float32).astype(
            jnp.bfloat16
        ),
        "mp",
        0,
    )
    token_start = lax.axis_index("mp") * token_share
    own_first = lax.dynamic_slice_in_dim(first_sum, token_start, token_share, 1).transpose(1, 0, 2)
    second_sum = own_first + gate_m[None] * mlp
    fin = (layer_norm(second_sum) * (1.0 + scale_f[None]) + shift_f[None]).astype(jnp.bfloat16)
    noise = jnp.einsum("tbd,do->bto", fin, out_weight, preferred_element_type=jnp.float32)
    noise = noise.reshape(2, pair_count, token_share * out_weight.shape[1])
    return noise[1] + guidance[0] * (noise[0] - noise[1])


def solution(mesh):
    torus = Mesh(
        mesh.devices.reshape(mesh.shape["group"], 8, 4, 2, mesh.shape["mp"]),
        ("group", "dp_0", "dp_1", "dp_2", "mp"),
    )
    placed = (
        P(GROUP_DP, None, None),
        P(GROUP_DP),
        P(GROUP_DP),
        P(GROUP_DP),
        P(),
        P(None, "mp"),
        P(None, "mp"),
        P("mp", DP),
        P("mp", None),
        P(None, DP, "mp"),
        P("mp", DP),
        P(DP, "mp"),
        P("mp", DP),
        P(),
    )
    return jax.shard_map(
        on_device, mesh=torus, in_specs=placed, out_specs=P(GROUP_DP, "mp"), check_vma=False
    )
```

profile of v0, /device:TPU:4, one launch (start us, length us, event | category | flops | bytes accessed | tf_op | source)
XLA Modules:
  0.0 341.8 jit_solution(6708045404015547400)
XLA Ops:
  7.4 1.6 copy.106
  10.3 1.0 constant_dynamic-slice_fusion
  11.4 1.0 constant_dynamic-slice_fusion.1
  13.2 0.7 broadcast_in_dim.50
  13.9 19.2 %all-to-all-start = ((bf16[64,2,288]{2,1,0:T(2,128)(2,1)}), bf16[64,2,288]{2,1,0:T(2,128)(2,1)S(1)}, u32[]{:S(2)}, u32[]{:S(2)}) async-start(bf16[64,2,288]{2,1,0:T(2,128)(2,1)} %broadcast_in_dim.50), calls=%async_computation | async-start | bytes 196608 | tf_op jit(solution)/shard_map/all_to_all | solution.py:15
  33.8 12.4 %all-to-all-done = bf16[64,2,288]{2,1,0:T(2,128)(2,1)S(1)} async-done(((bf16[64,2,288]{2,1,0:T(2,128)(2,1)}), bf16[64,2,288]{2,1,0:T(2,128)(2,1)S(1)}, u32[]{:S(2)}, u32[]{:S(2)}) %all-to-all-start) | async-done | bytes 73760 | tf_op jit(solution)/shard_map/all_to_all | solution.py:15
  46.3 1.1 convolution_convert_fusion.4
  47.4 0.7 broadcast_in_dim.84
  48.1 4.5 %all-to-all-start.1 = ((bf16[4,128,108]{1,2,0:T(8,128)(2,1)}), bf16[4,128,108]{1,2,0:T(8,128)(2,1)S(1)}, u32[]{:S(2)}, u32[]{:S(2)}) async-start(bf16[4,128,108]{1,2,0:T(8,128)(2,1)} %broadcast_in_dim.84), calls=%async_computation.1 | async-start | bytes 229376 | tf_op jit(solution)/shard_map/all_to_all | solution.py:15
  52.6 1.4 broadcast_select_fusion.1
  53.9 4.5 %all-to-all-done.1 = bf16[4,128,108]{1,2,0:T(8,128)(2,1)S(1)} async-done(((bf16[4,128,108]{1,2,0:T(8,128)(2,1)}), bf16[4,128,108]{1,2,0:T(8,128)(2,1)S(1)}, u32[]{:S(2)}, u32[]{:S(2)}) %all-to-all-start.1) | async-done | bytes 110624 | tf_op jit(solution)/shard_map/all_to_all | solution.py:15
  58.5 0.7 copy.104
  59.2 6.2 %all-to-all-start.2 = ((bf16[64,2,108]{2,1,0:T(2,128)(2,1)}), bf16[64,2,108]{2,1,0:T(2,128)(2,1)S(1)}, u32[]{:S(2)}, u32[]{:S(2)}) async-start(bf16[64,2,108]{2,1,0:T(2,128)(2,1)} %bitcast.7), calls=%async_computation.2 | async-start | bytes 65536 | tf_op jit(solution)/shard_map/all_to_all | solution.py:100
  65.6 12.4 %all-to-all-done.2 = bf16[64,2,108]{2,1,0:T(2,128)(2,1)S(1)} async-done(((bf16[64,2,108]{2,1,0:T(2,128)(2,1)}), bf16[64,2,108]{2,1,0:T(2,128)(2,1)S(1)}, u32[]{:S(2)}, u32[]{:S(2)}) %all-to-all-start.2) | async-done | bytes 27680 | tf_op jit(solution)/shard_map/all_to_all | solution.py:100
  78.0 1.1 broadcast_in_dim.85
  79.1 7.2 %all-to-all-start.3 = ((bf16[64,288,18]{1,2,0:T(8,128)(2,1)}), bf16[64,288,18]{1,2,0:T(8,128)(2,1)}, u32[]{:S(2)}, u32[]{:S(2)}) async-start(bf16[64,288,18]{1,2,0:T(8,128)(2,1)} %broadcast_in_dim.85), calls=%async_computation.3 | async-start | bytes 2359296 | tf_op jit(solution)/shard_map/all_to_all | solution.py:15
  87.1 1.7 fusion.16
  88.8 30.6 %all-to-all-done.3 = bf16[64,288,18]{1,2,0:T(8,128)(2,1)} async-done(((bf16[64,288,18]{1,2,0:T(8,128)(2,1)}), bf16[64,288,18]{1,2,0:T(8,128)(2,1)}, u32[]{:S(2)}, u32[]{:S(2)}) %all-to-all-start.3) | async-done | bytes 663584 | tf_op jit(solution)/shard_map/all_to_all | solution.py:15
  119.4 1.6 reshape.262
  121.0 51.8 %all-gather.8.cloned.1.call-done = bf16[3,1152,288]{2,0,1:T(4,128)(2,1)} async-done(((bf16[3,18,288]{2,0,1:T(4,128)(2,1)}), bf16[3,1152,288]{2,0,1:T(4,128)(2,1)}) %all-gather.8.cloned.1.call-update) | async-done | bytes 1990672 | tf_op jit(solution)/shard_map/all_gather | solution.py:117
  172.8 3.7 %fusion.26 = bf16[3,512,288]{1,2,0:T(8,128)(2,1)S(1)} fusion(bf16[3,1152,288]{2,0,1:T(4,128)(2,1)} %all-gather.8.cloned.1.call-done, bf16[512,1152]{1,0:T(8,128)(2,1)} %fusion.16), kind=kOutput, calls=%fused_computation.41 | convolution fusion | flops 1019658240 | bytes 4055040 | tf_op jit(solution)/shard_map/rd,kdc->krc/dot_general | solution.py:114
  176.6 0.9 fusion.62
  177.5 1.7 reshape_squeeze.10
  179.3 1.7 reshape_squeeze.11
  181.0 1.8 reshape_squeeze.9
  182.8 3.2 fusion.65
  186.0 2.0 fusion.30
  188.4 2.0 convolution_convert_fusion.2
  190.4 9.3 %all-gather = bf16[2,18,1152]{2,1,0:T(8,128)(2,1)S(1)} all-gather(bf16[1,18,1152]{2,1,0:T(8,128)(2,1)S(1)} %bitcast.125), channel_id=1, replica_groups=mesh['group'=2,'dp_0'=8,'dp_1'=4,'dp_2'=2,'mp'=4] {'dp_2'}, dimensions={0}, use_global_device_ids=true | all-gather | bytes 124416 | tf_op jit(solution)/shard_map/all_gather | solution.py:36
  199.8 11.3 %all-gather.1 = bf16[4,36,1152]{2,1,0:T(8,128)(2,1)S(1)} all-gather(bf16[1,36,1152]{2,1,0:T(8,128)(2,1)S(1)} %reshape.323), channel_id=1, replica_groups=mesh['group'=2,'dp_0'=8,'dp_1'=4,'dp_2'=2,'mp'=4] {'dp_1'}, dimensions={0}, use_global_device_ids=true | all-gather | bytes 414720 | tf_op jit(solution)/shard_map/all_gather | solution.py:36
  211.0 0.8 reshape.324
  211.9 10.3 %all-gather.2 = bf16[2,18,1152]{2,1,0:T(8,128)(2,1)S(1)} all-gather(bf16[1,18,1152]{2,1,0:T(8,128)(2,1)S(1)} %bitcast.126), channel_id=1, replica_groups=mesh['group'=2,'dp_0'=8,'dp_1'=4,'dp_2'=2,'mp'=4] {'dp_2'}, dimensions={0}, use_global_device_ids=true | all-gather | bytes 124416 | tf_op jit(solution)/shard_map/all_gather | solution.py:36
  222.2 12.4 %all-gather.3 = bf16[4,36,1152]{2,1,0:T(8,128)(2,1)S(1)} all-gather(bf16[1,36,1152]{2,1,0:T(8,128)(2,1)S(1)} %reshape.327), channel_id=1, replica_groups=mesh['group'=2,'dp_0'=8,'dp_1'=4,'dp_2'=2,'mp'=4] {'dp_1'}, dimensions={0}, use_global_device_ids=true | all-gather | bytes 414720 | tf_op jit(solution)/shard_map/all_gather | solution.py:36
  234.7 0.8 reshape.328
  235.9 0.6 broadcast_in_dim.86
  236.5 3.4 %all-to-all-start.5 = ((bf16[4,2,2304]{2,1,0:T(2,128)(2,1)}), bf16[4,2,2304]{2,1,0:T(2,128)(2,1)S(1)}, u32[]{:S(2)}, u32[]{:S(2)}) async-start(bf16[4,2,2304]{2,1,0:T(2,128)(2,1)} %broadcast_in_dim.86), calls=%async_computation.5 | async-start | bytes 73728 | tf_op jit(solution)/shard_map/all_to_all | solution.py:15
  240.0 21.1 %all-reduce.2.cloned.1.call-done = bf16[512,1152]{1,0:T(8,128)(2,1)} async-done(((bf16[512,1152]{1,0:T(8,128)(2,1)}), bf16[512,1152]{1,0:T(8,128)(2,1)}) %all-reduce.2.cloned.1.call-update) | async-done | bytes 1179664 | tf_op jit(solution)/shard_map/psum | solution.py:133
  261.1 1.7 fusion.60
  262.8 1.4 copy-done.1
  264.9 2.0 fusion.12
  266.9 4.0 %fusion.11 = bf16[512,1152]{1,0:T(8,128)(2,1)S(1)} fusion(bf16[512,1152]{1,0:T(8,128)(2,1)} %fusion.12, bf16[1152,1152]{1,0:T(8,128)(2,1)} %all-gather.10.cloned.1.call-done), kind=kOutput, calls=%fused_computation.15 | convolution fusion | flops 1364262912 | bytes 5013504 | tf_op jit(solution)/shard_map/dot_general | solution.py:144
  271.0 25.5 %all-gather.12.cloned.1.call-done = bf16[1152,1152]{0,1:T(8,128)(2,1)} async-done(((bf16[1152,144]{0,1:T(8,128)(2,1)}), bf16[1152,1152]{0,1:T(8,128)(2,1)}) %all-gather.12.cloned.1.call-update) | async-done | bytes 2654224 | tf_op jit(solution)/shard_map/all_gather | solution.py:36
  296.4 3.6 %convolution_convert_fusion.1 = bf16[2,256,1152]{2,1,0:T(8,128)(2,1)S(1)} fusion(bf16[2,256,1152]{2,1,0:T(8,128)(2,1)S(1)} %bitcast.131, bf16[1152,1152]{0,1:T(8,128)(2,1)} %all-gather.12.cloned.1.call-done), kind=kOutput, calls=%fused_computation.3 | convolution fusion | flops 1359544320 | bytes 5013504 | tf_op jit(solution)/shard_map/btf,fd->tbd/dot_general | solution.py:153
  300.0 1.1 copy.113
  301.2 4.8 %all-to-all-start.4 = ((bf16[4,64,2,1152]{3,1,2,0:T(8,128)(2,1)}), bf16[4,64,2,1152]{3,1,2,0:T(8,128)(2,1)S(1)}, u32[]{:S(2)}, u32[]{:S(2)}) async-start(bf16[4,64,2,1152]{3,1,2,0:T(8,128)(2,1)} %copy.113), calls=%async_computation.4 | async-start | bytes 2359296 | tf_op jit(solution)/shard_map/all_to_all | solution.py:48
  306.7 24.8 %all-to-all-done.4 = bf16[4,64,2,1152]{3,1,2,0:T(8,128)(2,1)S(1)} async-done(((bf16[4,64,2,1152]{3,1,2,0:T(8,128)(2,1)}), bf16[4,64,2,1152]{3,1,2,0:T(8,128)(2,1)S(1)}, u32[]{:S(2)}, u32[]{:S(2)}) %all-to-all-start.4) | async-done | bytes 1179680 | tf_op jit(solution)/shard_map/all_to_all | solution.py:48
  331.6 1.2 fusion.59
  333.8 0.6 multiply_add_fusion
  (67 shorter events, 4.6 us)
Async XLA Ops:
  7.4 228.2 %copy-start = (bf16[288,2304]{1,0:T(8,128)(2,1)S(1)}, bf16[288,2304]{1,0:T(8,128)(2,1)}, u32[]{:S(2)}) copy-start(bf16[288,2304]{1,0:T(8,128)(2,1)} %param.22) | copy-start | bytes 3981316
  7.4 165.5 %all-gather.8.cloned.1.call-start = ((), (), s32[]{:S(2)}) async-start(), calls=%async_computation.6 | async-start | bytes 3594240 | tf_op jit(solution)/shard_map/all_gather | solution.py:117
  12.7 0.6 copy-start.6
  13.9 64.1 %copy-start.5 = (bf16[288,18]{0,1:T(8,128)(2,1)S(1)}, bf16[288,18]{0,1:T(8,128)(2,1)}, u32[]{:S(2)}) copy-start(bf16[288,18]{0,1:T(8,128)(2,1)} %param.24) | copy-start | bytes 31108
  13.9 32.3 %all-to-all-start = ((bf16[64,2,288]{2,1,0:T(2,128)(2,1)}), bf16[64,2,288]{2,1,0:T(2,128)(2,1)S(1)}, u32[]{:S(2)}, u32[]{:S(2)}) async-start(bf16[64,2,288]{2,1,0:T(2,128)(2,1)} %broadcast_in_dim.50), calls=%async_computation | async-start | bytes 196608 | tf_op jit(solution)/shard_map/all_to_all | solution.py:15
  48.1 10.4 %all-to-all-start.1 = ((bf16[4,128,108]{1,2,0:T(8,128)(2,1)}), bf16[4,128,108]{1,2,0:T(8,128)(2,1)S(1)}, u32[]{:S(2)}, u32[]{:S(2)}) async-start(bf16[4,128,108]{1,2,0:T(8,128)(2,1)} %broadcast_in_dim.84), calls=%async_computation.1 | async-start | bytes 229376 | tf_op jit(solution)/shard_map/all_to_all | solution.py:15
  59.2 18.8 %all-to-all-start.2 = ((bf16[64,2,108]{2,1,0:T(2,128)(2,1)}), bf16[64,2,108]{2,1,0:T(2,128)(2,1)S(1)}, u32[]{:S(2)}, u32[]{:S(2)}) async-start(bf16[64,2,108]{2,1,0:T(2,128)(2,1)} %bitcast.7), calls=%async_computation.2 | async-start | bytes 65536 | tf_op jit(solution)/shard_map/all_to_all | solution.py:100
  79.1 40.3 %all-to-all-start.3 = ((bf16[64,288,18]{1,2,0:T(8,128)(2,1)}), bf16[64,288,18]{1,2,0:T(8,128)(2,1)}, u32[]{:S(2)}, u32[]{:S(2)}) async-start(bf16[64,288,18]{1,2,0:T(8,128)(2,1)} %broadcast_in_dim.85), calls=%async_computation.3 | async-start | bytes 2359296 | tf_op jit(solution)/shard_map/all_to_all | solution.py:15
  86.3 174.8 %all-reduce.2.cloned.1.call-start = ((), (), s32[]{:S(2)}) async-start(), calls=%async_computation.7 | async-start | bytes 2359296 | tf_op jit(solution)/shard_map/psum | solution.py:133
  188.0 2.4 copy-start.3
  188.4 23.6 %copy-start.4 = (bf16[1152,18]{0,1:T(8,128)(2,1)S(1)}, bf16[1152,18]{0,1:T(8,128)(2,1)}, u32[]{:S(2)}) copy-start(bf16[1152,18]{0,1:T(8,128)(2,1)} %param.26) | copy-start | bytes 124420
  190.3 45.2 %copy-start.7 = (bf16[2,288]{1,0:T(2,128)(2,1)S(1)}, bf16[2,288]{1,0:T(2,128)(2,1)}, u32[]{:S(2)}) copy-start(bf16[2,288]{1,0:T(2,128)(2,1)} %copy-done.6) | copy-start | bytes 3460
  190.4 76.6 %all-gather.10.cloned.1.call-start = ((), (), s32[]{:S(2)}) async-start(), calls=%async_computation.8 | async-start | bytes 2985984 | tf_op jit(solution)/shard_map/all_gather | solution.py:36
  211.9 84.6 %all-gather.12.cloned.1.call-start = ((), (), s32[]{:S(2)}) async-start(), calls=%async_computation.9 | async-start | bytes 2985984 | tf_op jit(solution)/shard_map/all_gather | solution.py:36
  236.5 64.7 %all-to-all-start.5 = ((bf16[4,2,2304]{2,1,0:T(2,128)(2,1)}), bf16[4,2,2304]{2,1,0:T(2,128)(2,1)S(1)}, u32[]{:S(2)}, u32[]{:S(2)}) async-start(bf16[4,2,2304]{2,1,0:T(2,128)(2,1)} %broadcast_in_dim.86), calls=%async_computation.5 | async-start | bytes 73728 | tf_op jit(solution)/shard_map/all_to_all | solution.py:15
  262.8 1.4 copy-start.1
  262.8 2.1 copy-start.2
  301.2 30.3 %all-to-all-start.4 = ((bf16[4,64,2,1152]{3,1,2,0:T(8,128)(2,1)}), bf16[4,64,2,1152]{3,1,2,0:T(8,128)(2,1)S(1)}, u32[]{:S(2)}, u32[]{:S(2)}) async-start(bf16[4,64,2,1152]{3,1,2,0:T(8,128)(2,1)} %copy.113), calls=%async_computation.4 | async-start | bytes 2359296 | tf_op jit(solution)/shard_map/all_to_all | solution.py:48
  305.9 27.1 %copy-start.8 = (bf16[1152,16]{0,1:T(8,128)(2,1)S(1)}, bf16[1152,16]{0,1:T(8,128)(2,1)}, u32[]{:S(2)}) copy-start(bf16[1152,16]{0,1:T(8,128)(2,1)} %param.27) | copy-start | bytes 110596
Sparse Core Ops, SparseCore 0:
  12.5 160.2 all-gather.7
  190.5 70.5 all-reduce.1
Sparse Core Ops, SparseCore 1:
  212.0 38.8 all-gather.9
  252.8 43.6 all-gather.11
where the time goes:
time: 343 us; the launch traced here: 342 us
  waiting for transfers between devices  183 us (53%)
  starting transfers between devices  45.4 us (13%)
  blocking collectives  43.3 us (13%)
  local copies, waits for them, and re-layouts  21.6 us (6%)
  matrix products  20.2 us (6%)
  between operations  17.8 us (5%)
  other arithmetic  10.3 us (3%)
    all_gather x1, waiting for transfers between devices, on_device(): lax.all_gather(qkv_weight, DP, axis=1, tiled=True)  51.8 us
    all_to_all x4, waiting for transfers between devices, from_everyone(): lax.all_to_all(jnp.broadcast_to(x[None], (size, *x.shape)), axis, 0, 0, t...  47.6 us
    all_gather x4, blocking collectives, gathered_by_axis(): x = lax.all_gather(x, axis, axis=dim, tiled=True)  43.3 us
    all_to_all x4, starting transfers between devices, from_everyone(): lax.all_to_all(jnp.broadcast_to(x[None], (size, *x.shape)), axis, 0, 0, t...  34.3 us
    all_gather x2, waiting for transfers between devices, gathered_by_axis(): x = lax.all_gather(x, axis, axis=dim, tiled=True)  25.5 us
    all_to_all x1, waiting for transfers between devices, sum_at_owner(): pieces = lax.all_to_all(cut_along(x, dim, size), axis, 0, 0, tiled=True)  24.8 us
    psum x1, waiting for transfers between devices, on_device(): lax.psum(attn_part.astype(jnp.bfloat16), 'mp').astype(jnp.float32)  21.1 us
    all_to_all x1, waiting for transfers between devices, on_device(): lax.all_to_all(summed.astype(jnp.bfloat16), DP, split_axis=0, concat_axis...  12.4 us
  transfers between devices with their start and end apart: 10, of which 8 were waited for; matrix products, arithmetic and copies ran while one was open for 8% of the time, Pallas kernels for 0%

commit v1 on v0

--- a/solution.py
+++ b/solution.py
@@ -114,7 +114,7 @@
     qkv = jnp.einsum(
         "rd,kdc->krc",
         columns,
-        lax.all_gather(qkv_weight, DP, axis=1, tiled=True),
+        jnp.concatenate(lax.all_gather(qkv_weight, DP), axis=1),
         preferred_element_type=jnp.float32,
     ).astype(jnp.bfloat16)
     query = qkv[0].reshape(image_count, tokens, local_heads, head_dim)

time: 343 us -> 358 us (1.044)
  local copies, waits for them, and re-layouts: 21.6 us -> 29.9 us
  waiting for transfers between devices: 183 us -> 191 us
    all_gather x1, waiting for transfers between devices: 51.8 us -> 58.3 us  [on_device(): lax.all_gather(qkv_weight, DP)]
    reshape x0 -> x1, local copies, waits for them, and re-layouts: none -> 5.65 us  [on_device(): jnp.concatenate(lax.all_gather(qkv_weight, DP), axis=1)]
    all_gather x0 -> x1, local copies, waits for them, and re-layouts: none -> 4.16 us  [on_device(): lax.all_gather(qkv_weight, DP)]
where the time goes in v1:
time: 358 us; the launch traced here: 357 us
  waiting for transfers between devices  191 us (53%)
  starting transfers between devices  45.4 us (13%)
  blocking collectives  43.3 us (12%)
  local copies, waits for them, and re-layouts  29.9 us (8%)
  matrix products  19.1 us (5%)
  between operations  17.8 us (5%)
  other arithmetic  10.1 us (3%)
    all_gather x1, waiting for transfers between devices, on_device(): lax.all_gather(qkv_weight, DP)  58.3 us
    all_to_all x4, waiting for transfers between devices, from_everyone(): lax.all_to_all(jnp.broadcast_to(x[None], (size, *x.shape)), axis, 0, 0, t...  48.4 us
    all_gather x4, blocking collectives, gathered_by_axis(): x = lax.all_gather(x, axis, axis=dim, tiled=True)  43.3 us
    all_to_all x4, starting transfers between devices, from_everyone(): lax.all_to_all(jnp.broadcast_to(x[None], (size, *x.shape)), axis, 0, 0, t...  34.2 us
    all_gather x2, waiting for transfers between devices, gathered_by_axis(): x = lax.all_gather(x, axis, axis=dim, tiled=True)  25.6 us
    all_to_all x1, waiting for transfers between devices, sum_at_owner(): pieces = lax.all_to_all(cut_along(x, dim, size), axis, 0, 0, tiled=True)  24.8 us
    psum x1, waiting for transfers between devices, on_device(): lax.psum(attn_part.astype(jnp.bfloat16), 'mp').astype(jnp.float32)  21.1 us
    all_to_all x1, waiting for transfers between devices, on_device(): lax.all_to_all(summed.astype(jnp.bfloat16), DP, split_axis=0, concat_axis...  12.2 us
  transfers between devices with their start and end apart: 10, of which 8 were waited for; matrix products, arithmetic and copies ran while one was open for 8% of the time, Pallas kernels for 0%

profile of v1, /device:TPU:4, one launch (start us, length us, event | category | flops | bytes accessed | tf_op | source)
XLA Modules:
  0.0 356.7 jit_solution(16617043603877623151)
XLA Ops:
  7.4 0.7 all-gather.13.cloned.1.call-update
  9.4 1.1 constant_dynamic-slice_fusion
  10.6 1.0 constant_dynamic-slice_fusion.1
  12.4 0.7 broadcast_in_dim.50
  13.1 19.1 %all-to-all-start = ((bf16[64,2,288]{2,1,0:T(2,128)(2,1)}), bf16[64,2,288]{2,1,0:T(2,128)(2,1)S(1)}, u32[]{:S(2)}, u32[]{:S(2)}) async-start(bf16[64,2,288]{2,1,0:T(2,128)(2,1)} %broadcast_in_dim.50), calls=%async_computation | async-start | bytes 196608 | tf_op jit(solution)/shard_map/all_to_all | solution.py:15
  32.8 1.4 broadcast_select_fusion.1
  34.4 10.7 %all-to-all-done = bf16[64,2,288]{2,1,0:T(2,128)(2,1)S(1)} async-done(((bf16[64,2,288]{2,1,0:T(2,128)(2,1)}), bf16[64,2,288]{2,1,0:T(2,128)(2,1)S(1)}, u32[]{:S(2)}, u32[]{:S(2)}) %all-to-all-start) | async-done | bytes 73760 | tf_op jit(solution)/shard_map/all_to_all | solution.py:15
  45.5 0.7 broadcast_in_dim.84
  46.1 4.6 %all-to-all-start.1 = ((bf16[4,128,108]{1,2,0:T(8,128)(2,1)}), bf16[4,128,108]{1,2,0:T(8,128)(2,1)S(1)}, u32[]{:S(2)}, u32[]{:S(2)}) async-start(bf16[4,128,108]{1,2,0:T(8,128)(2,1)} %broadcast_in_dim.84), calls=%async_computation.1 | async-start | bytes 229376 | tf_op jit(solution)/shard_map/all_to_all | solution.py:15
  50.7 5.9 %all-to-all-done.1 = bf16[4,128,108]{1,2,0:T(8,128)(2,1)S(1)} async-done(((bf16[4,128,108]{1,2,0:T(8,128)(2,1)}), bf16[4,128,108]{1,2,0:T(8,128)(2,1)S(1)}, u32[]{:S(2)}, u32[]{:S(2)}) %all-to-all-start.1) | async-done | bytes 110624 | tf_op jit(solution)/shard_map/all_to_all | solution.py:15
  56.6 0.7 copy.109
  57.3 6.2 %all-to-all-start.2 = ((bf16[64,2,108]{2,1,0:T(2,128)(2,1)}), bf16[64,2,108]{2,1,0:T(2,128)(2,1)S(1)}, u32[]{:S(2)}, u32[]{:S(2)}) async-start(bf16[64,2,108]{2,1,0:T(2,128)(2,1)} %bitcast.7), calls=%async_computation.2 | async-start | bytes 65536 | tf_op jit(solution)/shard_map/all_to_all | solution.py:100
  64.0 12.2 %all-to-all-done.2 = bf16[64,2,108]{2,1,0:T(2,128)(2,1)S(1)} async-done(((bf16[64,2,108]{2,1,0:T(2,128)(2,1)}), bf16[64,2,108]{2,1,0:T(2,128)(2,1)S(1)}, u32[]{:S(2)}, u32[]{:S(2)}) %all-to-all-start.2) | async-done | bytes 27680 | tf_op jit(solution)/shard_map/all_to_all | solution.py:100
  76.2 1.2 broadcast_in_dim.85
  77.3 7.2 %all-to-all-start.3 = ((bf16[64,288,18]{1,2,0:T(8,128)(2,1)}), bf16[64,288,18]{1,2,0:T(8,128)(2,1)}, u32[]{:S(2)}, u32[]{:S(2)}) async-start(bf16[64,288,18]{1,2,0:T(8,128)(2,1)} %broadcast_in_dim.85), calls=%async_computation.3 | async-start | bytes 2359296 | tf_op jit(solution)/shard_map/all_to_all | solution.py:15
  84.8 1.5 fusion.19
  86.3 31.8 %all-to-all-done.3 = bf16[64,288,18]{1,2,0:T(8,128)(2,1)} async-done(((bf16[64,288,18]{1,2,0:T(8,128)(2,1)}), bf16[64,288,18]{1,2,0:T(8,128)(2,1)}, u32[]{:S(2)}, u32[]{:S(2)}) %all-to-all-start.3) | async-done | bytes 663584 | tf_op jit(solution)/shard_map/all_to_all | solution.py:15
  118.1 1.6 reshape.324
  119.8 58.3 %all-gather.13.cloned.1.call-done = bf16[192,18,288]{2,1,0:T(8,128)(2,1)} async-done(((bf16[3,18,288]{2,1,0:T(8,128)(2,1)}), bf16[192,18,288]{2,1,0:T(8,128)(2,1)}) %all-gather.13.cloned.1.call-update) | async-done | bytes 1990672 | tf_op jit(solution)/shard_map/all_gather | solution.py:117
  178.0 4.2 %copy.154 = bf16[64,3,18,288]{3,2,0,1:T(8,128)(2,1)} copy(bf16[64,3,18,288]{3,2,1,0:T(8,128)(2,1)} %bitcast.113) | data formatting | bytes 3981312 | tf_op jit(solution)/shard_map/all_gather | solution.py:117
  182.2 5.6 %reshape.322 = bf16[3,1152,288]{2,1,0:T(8,128)(2,1)} reshape(bf16[3,64,18,288]{3,2,1,0:T(8,128)(2,1)} %bitcast.111) | data formatting | bytes 3981312 | tf_op jit(solution)/shard_map/reshape | solution.py:117
  187.9 3.5 fusion.21
  191.4 0.9 fusion.52
  192.3 1.7 reshape_squeeze.10
  194.0 1.7 reshape_squeeze.11
  195.8 1.8 reshape_squeeze.9
  197.5 3.2 fusion.55
  200.8 2.0 fusion.22
  203.2 2.0 convolution_convert_fusion.2
  205.2 9.3 %all-gather.1 = bf16[2,18,1152]{2,1,0:T(8,128)(2,1)S(1)} all-gather(bf16[1,18,1152]{2,1,0:T(8,128)(2,1)S(1)} %bitcast.120), channel_id=1, replica_groups=mesh['group'=2,'dp_0'=8,'dp_1'=4,'dp_2'=2,'mp'=4] {'dp_2'}, dimensions={0}, use_global_device_ids=true | all-gather | bytes 124416 | tf_op jit(solution)/shard_map/all_gather | solution.py:36
  214.5 11.3 %all-gather.2 = bf16[4,36,1152]{2,1,0:T(8,128)(2,1)S(1)} all-gather(bf16[1,36,1152]{2,1,0:T(8,128)(2,1)S(1)} %reshape.386), channel_id=1, replica_groups=mesh['group'=2,'dp_0'=8,'dp_1'=4,'dp_2'=2,'mp'=4] {'dp_1'}, dimensions={0}, use_global_device_ids=true | all-gather | bytes 414720 | tf_op jit(solution)/shard_map/all_gather | solution.py:36
  225.8 0.8 reshape.387
  226.7 10.3 %all-gather.3 = bf16[2,18,1152]{2,1,0:T(8,128)(2,1)S(1)} all-gather(bf16[1,18,1152]{2,1,0:T(8,128)(2,1)S(1)} %bitcast.121), channel_id=1, replica_groups=mesh['group'=2,'dp_0'=8,'dp_1'=4,'dp_2'=2,'mp'=4] {'dp_2'}, dimensions={0}, use_global_device_ids=true | all-gather | bytes 124416 | tf_op jit(solution)/shard_map/all_gather | solution.py:36
  237.0 12.4 %all-gather.4 = bf16[4,36,1152]{2,1,0:T(8,128)(2,1)S(1)} all-gather(bf16[1,36,1152]{2,1,0:T(8,128)(2,1)S(1)} %reshape.390), channel_id=1, replica_groups=mesh['group'=2,'dp_0'=8,'dp_1'=4,'dp_2'=2,'mp'=4] {'dp_1'}, dimensions={0}, use_global_device_ids=true | all-gather | bytes 414720 | tf_op jit(solution)/shard_map/all_gather | solution.py:36
  249.5 0.8 reshape.391
  250.6 0.6 broadcast_in_dim.86
  251.3 3.4 all-to-all-start.5
  254.7 21.1 %all-reduce.2.cloned.1.call-done = bf16[512,1152]{1,0:T(8,128)(2,1)} async-done(((bf16[512,1152]{1,0:T(8,128)(2,1)}), bf16[512,1152]{1,0:T(8,128)(2,1)}) %all-reduce.2.cloned.1.call-update) | async-done | bytes 1179664 | tf_op jit(solution)/shard_map/psum | solution.py:133
  275.8 1.7 fusion.51
  277.6 1.4 copy-done.1
  279.7 2.0 fusion.10
  281.7 4.0 %fusion.9 = bf16[512,1152]{1,0:T(8,128)(2,1)S(1)} fusion(bf16[512,1152]{1,0:T(8,128)(2,1)} %fusion.10, bf16[1152,1152]{1,0:T(8,128)(2,1)} %all-gather.9.cloned.1.call-done), kind=kOutput, calls=%fused_computation.14 | convolution fusion | flops 1364262912 | bytes 5013504 | tf_op jit(solution)/shard_map/dot_general | solution.py:144
  285.7 25.6 %all-gather.11.cloned.1.call-done = bf16[1152,1152]{0,1:T(8,128)(2,1)} async-done(((bf16[1152,144]{0,1:T(8,128)(2,1)}), bf16[1152,1152]{0,1:T(8,128)(2,1)}) %all-gather.11.cloned.1.call-update) | async-done | bytes 2654224 | tf_op jit(solution)/shard_map/all_gather | solution.py:36
  311.3 3.6 %convolution_convert_fusion.1 = bf16[2,256,1152]{2,1,0:T(8,128)(2,1)S(1)} fusion(bf16[2,256,1152]{2,1,0:T(8,128)(2,1)S(1)} %bitcast.124, bf16[1152,1152]{0,1:T(8,128)(2,1)} %all-gather.11.cloned.1.call-done), kind=kOutput, calls=%fused_computation.4 | convolution fusion | flops 1359544320 | bytes 5013504 | tf_op jit(solution)/shard_map/btf,fd->tbd/dot_general | solution.py:153
  314.9 1.1 copy.118
  316.0 4.8 %all-to-all-start.4 = ((bf16[4,64,2,1152]{3,1,2,0:T(8,128)(2,1)}), bf16[4,64,2,1152]{3,1,2,0:T(8,128)(2,1)S(1)}, u32[]{:S(2)}, u32[]{:S(2)}) async-start(bf16[4,64,2,1152]{3,1,2,0:T(8,128)(2,1)} %copy.118), calls=%async_computation.4 | async-start | bytes 2359296 | tf_op jit(solution)/shard_map/all_to_all | solution.py:48
  321.6 24.8 %all-to-all-done.4 = bf16[4,64,2,1152]{3,1,2,0:T(8,128)(2,1)S(1)} async-done(((bf16[4,64,2,1152]{3,1,2,0:T(8,128)(2,1)}), bf16[4,64,2,1152]{3,1,2,0:T(8,128)(2,1)S(1)}, u32[]{:S(2)}, u32[]{:S(2)}) %all-to-all-start.4) | async-done | bytes 1179680 | tf_op jit(solution)/shard_map/all_to_all | solution.py:48
  346.5 1.2 fusion.50
  (68 shorter events, 5.5 us)
Async XLA Ops:
  7.4 243.0 %copy-start = (bf16[288,2304]{1,0:T(8,128)(2,1)S(1)}, bf16[288,2304]{1,0:T(8,128)(2,1)}, u32[]{:S(2)}) copy-start(bf16[288,2304]{1,0:T(8,128)(2,1)} %param.22) | copy-start | bytes 3981316
  7.4 170.7 %all-gather.13.cloned.1.call-start = ((), (), s32[]{:S(2)}) async-start(), calls=%async_computation.9 | async-start | bytes 3594240 | tf_op jit(solution)/shard_map/all_gather | solution.py:117
  9.4 35.9 %copy-start.3 = (bf16[288,108]{1,0:T(8,128)(2,1)S(1)}, bf16[288,108]{1,0:T(8,128)(2,1)}, u32[]{:S(2)}) copy-start(bf16[288,108]{1,0:T(8,128)(2,1)} %param.21) | copy-start | bytes 186628
  11.8 0.6 copy-start.7
  13.1 32.1 %all-to-all-start = ((bf16[64,2,288]{2,1,0:T(2,128)(2,1)}), bf16[64,2,288]{2,1,0:T(2,128)(2,1)S(1)}, u32[]{:S(2)}, u32[]{:S(2)}) async-start(bf16[64,2,288]{2,1,0:T(2,128)(2,1)} %broadcast_in_dim.50), calls=%async_computation | async-start | bytes 196608 | tf_op jit(solution)/shard_map/all_to_all | solution.py:15
  32.8 43.3 %copy-start.6 = (bf16[288,18]{0,1:T(8,128)(2,1)S(1)}, bf16[288,18]{0,1:T(8,128)(2,1)}, u32[]{:S(2)}) copy-start(bf16[288,18]{0,1:T(8,128)(2,1)} %param.24) | copy-start | bytes 31108
  46.1 10.5 %all-to-all-start.1 = ((bf16[4,128,108]{1,2,0:T(8,128)(2,1)}), bf16[4,128,108]{1,2,0:T(8,128)(2,1)S(1)}, u32[]{:S(2)}, u32[]{:S(2)}) async-start(bf16[4,128,108]{1,2,0:T(8,128)(2,1)} %broadcast_in_dim.84), calls=%async_computation.1 | async-start | bytes 229376 | tf_op jit(solution)/shard_map/all_to_all | solution.py:15
  57.3 18.8 %all-to-all-start.2 = ((bf16[64,2,108]{2,1,0:T(2,128)(2,1)}), bf16[64,2,108]{2,1,0:T(2,128)(2,1)S(1)}, u32[]{:S(2)}, u32[]{:S(2)}) async-start(bf16[64,2,108]{2,1,0:T(2,128)(2,1)} %bitcast.7), calls=%async_computation.2 | async-start | bytes 65536 | tf_op jit(solution)/shard_map/all_to_all | solution.py:100
  77.3 40.8 %all-to-all-start.3 = ((bf16[64,288,18]{1,2,0:T(8,128)(2,1)}), bf16[64,288,18]{1,2,0:T(8,128)(2,1)}, u32[]{:S(2)}, u32[]{:S(2)}) async-start(bf16[64,288,18]{1,2,0:T(8,128)(2,1)} %broadcast_in_dim.85), calls=%async_computation.3 | async-start | bytes 2359296 | tf_op jit(solution)/shard_map/all_to_all | solution.py:15
  84.5 191.3 %all-reduce.2.cloned.1.call-start = ((), (), s32[]{:S(2)}) async-start(), calls=%async_computation.6 | async-start | bytes 2359296 | tf_op jit(solution)/shard_map/psum | solution.py:133
  202.8 2.4 copy-start.4
  203.1 23.6 %copy-start.5 = (bf16[1152,18]{0,1:T(8,128)(2,1)S(1)}, bf16[1152,18]{0,1:T(8,128)(2,1)}, u32[]{:S(2)}) copy-start(bf16[1152,18]{0,1:T(8,128)(2,1)} %param.26) | copy-start | bytes 124420
  205.1 45.2 %copy-start.8 = (bf16[2,288]{1,0:T(2,128)(2,1)S(1)}, bf16[2,288]{1,0:T(2,128)(2,1)}, u32[]{:S(2)}) copy-start(bf16[2,288]{1,0:T(2,128)(2,1)} %copy-done.7) | copy-start | bytes 3460
  205.1 76.6 %all-gather.9.cloned.1.call-start = ((), (), s32[]{:S(2)}) async-start(), calls=%async_computation.7 | async-start | bytes 2985984 | tf_op jit(solution)/shard_map/all_gather | solution.py:36
  226.6 84.7 %all-gather.11.cloned.1.call-start = ((), (), s32[]{:S(2)}) async-start(), calls=%async_computation.8 | async-start | bytes 2985984 | tf_op jit(solution)/shard_map/all_gather | solution.py:36
  251.3 64.7 %all-to-all-start.5 = ((bf16[4,2,2304]{2,1,0:T(2,128)(2,1)}), bf16[4,2,2304]{2,1,0:T(2,128)(2,1)S(1)}, u32[]{:S(2)}, u32[]{:S(2)}) async-start(bf16[4,2,2304]{2,1,0:T(2,128)(2,1)} %broadcast_in_dim.86), calls=%async_computation.5 | async-start | bytes 73728 | tf_op jit(solution)/shard_map/all_to_all | solution.py:15
  277.6 1.4 copy-start.1
  277.6 2.1 copy-start.2
  316.0 30.3 %all-to-all-start.4 = ((bf16[4,64,2,1152]{3,1,2,0:T(8,128)(2,1)}), bf16[4,64,2,1152]{3,1,2,0:T(8,128)(2,1)S(1)}, u32[]{:S(2)}, u32[]{:S(2)}) async-start(bf16[4,64,2,1152]{3,1,2,0:T(8,128)(2,1)} %copy.118), calls=%async_computation.4 | async-start | bytes 2359296 | tf_op jit(solution)/shard_map/all_to_all | solution.py:48
  320.8 27.1 %copy-start.9 = (bf16[1152,16]{0,1:T(8,128)(2,1)S(1)}, bf16[1152,16]{0,1:T(8,128)(2,1)}, u32[]{:S(2)}) copy-start(bf16[1152,16]{0,1:T(8,128)(2,1)} %param.27) | copy-start | bytes 110596
Sparse Core Ops, SparseCore 0:
  12.5 165.4 all-gather.12
  205.3 70.5 all-reduce.1
Sparse Core Ops, SparseCore 1:
  226.7 38.6 all-gather.8
  267.4 43.9 all-gather.10
